TPU v7x, 32 devices: a whole 2x2x4 slice. The times are simulated.
32 devices in a mesh: dp: 8 (over y, x, core), tensor: 4 (over z).
Axes of the slice: x: 2, y: 2, z: 4, core: 2. Of those that a mesh axis runs over, the one named last changes fastest.
Arguments:
- tokens: bfloat16 [128, 196, 768], P(('dp', 'tensor')), may hold values from -6 to 6
- space_gain: float32 [768], replicated, may hold values from 0.5 to 1.5
- space_shift: float32 [768], replicated, may hold values from -3 to 3
- space_inproj: bfloat16 [768, 3, 768], P(None, None, 'tensor'), may hold values from -0.21875 to 0.21875
- space_bias: bfloat16 [2, 768], P(None, 'tensor'), may hold values from -3 to 3
- space_outproj: bfloat16 [768, 768], P('tensor'), may hold values from -1.75 to 1.75
- space_outbias: bfloat16 [768], replicated, may hold values from -3 to 3
- time_gain: float32 [768], replicated, may hold values from 0.5 to 1.5
- time_shift: float32 [768], replicated, may hold values from -3 to 3
- time_inproj: bfloat16 [768, 3, 768], P(None, None, 'tensor'), may hold values from -0.21875 to 0.21875
- time_bias: bfloat16 [2, 768], P(None, 'tensor'), may hold values from -3 to 3
- time_outproj: bfloat16 [768, 768], P('tensor'), may hold values from -0.5 to 0.5
- time_outbias: bfloat16 [768], replicated, may hold values from -3 to 3
- feed_gain: float32 [768], replicated, may hold values from 0.5 to 1.5
- feed_shift: float32 [768], replicated, may hold values from -3 to 3
- up_weight: bfloat16 [3072, 768], P('tensor'), may hold values from -0.21875 to 0.21875
- up_bias: bfloat16 [3072], P('tensor'), may hold values from -3 to 3
- down_weight: bfloat16 [3072, 768], P('tensor'), may hold values from -0.15625 to 0.15625
- down_bias: bfloat16 [768], replicated, may hold values from -3 to 3
- cotangent: bfloat16 [128, 196, 768], P(('dp', 'tensor')), may hold values from -6 to 6
Outputs:
- layer_out: bfloat16 [128, 196, 768], P(('dp', 'tensor'))
- input_gradient: float32 [128, 196, 768], P(('dp', 'tensor'))
- space_gain_gradient: float32 [768], replicated
- space_shift_gradient: float32 [768], replicated
- space_inproj_gradient: float32 [768, 3, 768], P(None, None, 'tensor')
- space_bias_gradient: float32 [2, 768], P(None, 'tensor')
- space_outproj_gradient: float32 [768, 768], P('tensor')
- space_outbias_gradient: float32 [768], replicated
- time_gain_gradient: float32 [768], replicated
- time_shift_gradient: float32 [768], replicated
- time_inproj_gradient: float32 [768, 3, 768], P(None, None, 'tensor')
- time_bias_gradient: float32 [2, 768], P(None, 'tensor')
- time_outproj_gradient: float32 [768, 768], P('tensor')
- time_outbias_gradient: float32 [768], replicated
- feed_gain_gradient: float32 [768], replicated
- feed_shift_gradient: float32 [768], replicated
- up_weight_gradient: float32 [3072, 768], P('tensor')
- up_bias_gradient: float32 [3072], P('tensor')
- down_weight_gradient: float32 [3072, 768], P('tensor')
- down_bias_gradient: float32 [768], replicated
All inputs are finite; a program needn't handle non-finite values.
Results may differ from a plain program's by a relative error of at most 0.013.
The roundings to bfloat16 on the way count: a program that leaves them out, or rounds other values in their place, can miss the bound.
Values may be sent and summed in bfloat16 or wider, within the bound.
A program may use at most 192 MiB of HBM per device.

v0:
```python
import jax
import jax.numpy as jnp
from jax import lax
from jax.sharding import PartitionSpec as P

HS = 64
PATCH = 196
TIMES = 16
EPSILON = 1e-06
ROOT_HALF = 0.7071067811865476
INV_ROOT_TAU = 0.3989422804014327


def layer_norm(values, gain, shift):
    center = values - jnp.mean(values, axis=-1, keepdims=True)
    second = jnp.mean(center * center, axis=-1, keepdims=True)
    return center * lax.rsqrt(second + EPSILON) * gain + shift


def gelu_exact(values):
    return 0.5 * values * (1.0 + lax.erf(values * ROOT_HALF))


def gelu_slope(values):
    return (
        0.5 * (1.0 + lax.erf(values * ROOT_HALF))
        + values * jnp.exp(-0.5 * values * values) * INV_ROOT_TAU
    )


def head_forms(batch_first):
    if batch_first:
        return ("blhe", "bmhe", "bhlm")
    return ("lbhe", "mbhe", "bhlm")


def attend(queries, keys, values, batch_first):
    query_form, key_form, score_form = head_forms(batch_first)
    qk_scale = HS ** (-0.5)
    scores = (
        jnp.einsum(
            query_form + "," + key_form + "->" + score_form,
            queries,
            keys,
            preferred_element_type=jnp.float32,
        )
        * qk_scale
    )
    top = jnp.max(scores, axis=-1, keepdims=True)
    weights = jnp.exp(scores - top)
    total = jnp.sum(weights, axis=-1, keepdims=True)
    probs = (weights / total).astype(jnp.bfloat16)
    mixed = jnp.einsum(
        score_form + "," + key_form + "->" + query_form,
        probs,
        values,
        preferred_element_type=jnp.float32,
    )
    return (mixed, top + jnp.log(total))


def attend_back(queries, keys, values, log_total, mixed_grad, batch_first):
    query_form, key_form, score_form = head_forms(batch_first)
    qk_scale = HS ** (-0.5)
    to_scores = query_form + "," + key_form + "->" + score_form
    scores = jnp.einsum(to_scores, queries, keys, preferred_element_type=jnp.float32) * qk_scale
    probs = jnp.exp(scores - log_total)
    value_grad = jnp.einsum(
        score_form + "," + query_form + "->" + key_form,
        probs.astype(jnp.bfloat16),
        mixed_grad,
        preferred_element_type=jnp.float32,
    )
    prob_grad = jnp.einsum(to_scores, mixed_grad, values, preferred_element_type=jnp.float32)
    inner = jnp.sum(prob_grad * probs, axis=-1, keepdims=True)
    score_grad = (probs * (prob_grad - inner)).astype(jnp.bfloat16)
    query_grad = (
        jnp.einsum(
            score_form + "," + key_form + "->" + query_form,
            score_grad,
            keys,
            preferred_element_type=jnp.float32,
        )
        * qk_scale
    )
    key_grad = (
        jnp.einsum(
            score_form + "," + query_form + "->" + key_form,
            score_grad,
            queries,
            preferred_element_type=jnp.float32,
        )
        * qk_scale
    )
    return (query_grad, key_grad, value_grad)


def full_rows(shard):
    return lax.all_gather(shard, "tensor", axis=0, tiled=True)


def partial_rows(make_term, own_rows):
    return lax.psum_scatter(
        make_term(jnp.int32(0), own_rows * lax.axis_size("tensor")),
        "tensor",
        scatter_dimension=0,
        tiled=True,
    )


def to_patches(frame_major, times_local):
    width = frame_major.shape[-1]
    grouped = frame_major.reshape(times_local, -1, width)
    moved = lax.all_to_all(grouped, "dp", split_axis=1, concat_axis=0, tiled=True)
    return moved.reshape(TIMES, -1, width)


def to_frames(patch_major, times_local):
    width = patch_major.shape[-1]
    grouped = patch_major.reshape(lax.axis_size("dp") * times_local, -1, width)
    moved = lax.all_to_all(grouped, "dp", split_axis=0, concat_axis=1, tiled=True)
    return moved.reshape(-1, width)


def in_weights(inproj, bias_pair):
    width = inproj.shape[2]
    weight = inproj.reshape(inproj.shape[0], 3 * width)
    zero_part = jnp.zeros((width,), jnp.float32)
    bias = jnp.concatenate(
        [bias_pair[0].astype(jnp.float32), zero_part, bias_pair[1].astype(jnp.float32)]
    )
    return (weight, bias)


def attention_forward(resid, gain, shift, weight_set, outbias, temporal, times_local):
    inproj, bias_pair, outproj = weight_set
    normed, norm_pull = jax.vjp(layer_norm, resid, gain, shift)
    rows_in = full_rows(normed.astype(jnp.bfloat16))
    weight, bias = in_weights(inproj, bias_pair)
    width = inproj.shape[2]
    projected = (jnp.dot(rows_in, weight, preferred_element_type=jnp.float32) + bias).astype(
        jnp.bfloat16
    )
    heads_here = projected.shape[-1] // (3 * HS)
    if temporal:
        projected = to_patches(projected, times_local)
        split_heads = projected.reshape(TIMES, -1, 3, heads_here, HS)
    else:
        split_heads = projected.reshape(-1, PATCH, 3, heads_here, HS)
    mixed, log_total = attend(
        split_heads[:, :, 0], split_heads[:, :, 1], split_heads[:, :, 2], not temporal
    )
    if temporal:
        mixed_low = to_frames(
            mixed.astype(jnp.bfloat16).reshape(TIMES, -1, heads_here * HS), times_local
        )
    else:
        mixed_low = mixed.astype(jnp.bfloat16).reshape(-1, width)

    def out_term(start, count):
        return jnp.dot(
            lax.dynamic_slice_in_dim(mixed_low, start, count, 0),
            outproj,
            preferred_element_type=jnp.float32,
        )

    branch = partial_rows(out_term, resid.shape[0]) + outbias.astype(jnp.float32)
    kept = (norm_pull, rows_in, split_heads, log_total, mixed_low)
    return (resid + branch, kept)


def attention_backward(upstream, kept, weight_set, temporal, times_local):
    inproj, bias_pair, outproj = weight_set
    norm_pull, rows_in, split_heads, log_total, mixed_low = kept
    contract_rows = (((0,), (0,)), ((), ()))
    contract_cols = (((1,), (1,)), ((), ()))
    branch_low = upstream.astype(jnp.bfloat16)
    outbias_grad = jnp.sum(branch_low, axis=0, dtype=jnp.float32)
    branch_rows = full_rows(branch_low)
    outproj_grad = lax.dot_general(
        mixed_low, branch_rows, contract_rows, preferred_element_type=jnp.float32
    )
    mixed_grad = lax.dot_general(
        branch_rows, outproj, contract_cols, preferred_element_type=jnp.float32
    ).astype(jnp.bfloat16)
    width = inproj.shape[2]
    heads_here = split_heads.shape[3]
    if temporal:
        mixed_grad = to_patches(mixed_grad, times_local)
    mixed_grad = mixed_grad.reshape(split_heads.shape[0], split_heads.shape[1], heads_here, HS)
    query_grad, key_grad, value_grad = attend_back(
        split_heads[:, :, 0],
        split_heads[:, :, 1],
        split_heads[:, :, 2],
        log_total,
        mixed_grad,
        not temporal,
    )
    projected_grad = jnp.stack([query_grad, key_grad, value_grad], axis=2).astype(jnp.bfloat16)
    if temporal:
        projected_grad = to_frames(
            projected_grad.reshape(TIMES, -1, 3 * heads_here * HS), times_local
        )
    else:
        projected_grad = projected_grad.reshape(-1, 3 * width)
    column_sums = jnp.sum(projected_grad, axis=0, dtype=jnp.float32).reshape(3, width)
    bias_grad = jnp.stack([column_sums[0], column_sums[2]])
    weight = inproj.reshape(inproj.shape[0], 3 * width)
    inproj_grad = lax.dot_general(
        rows_in, projected_grad, contract_rows, preferred_element_type=jnp.float32
    ).reshape(inproj.shape)

    def in_term(start, count):
        return lax.dot_general(
            lax.dynamic_slice_in_dim(projected_grad, start, count, 0),
            weight,
            contract_cols,
            preferred_element_type=jnp.float32,
        )

    normed_grad = partial_rows(in_term, upstream.shape[0])
    resid_grad, gain_grad, shift_grad = norm_pull(normed_grad)
    return (
        upstream + resid_grad,
        (gain_grad, shift_grad, inproj_grad, bias_grad, outproj_grad, outbias_grad),
    )


def per_device(
    tokens,
    space_gain,
    space_shift,
    space_inproj,
    space_bias,
    space_outproj,
    space_outbias,
    time_gain,
    time_shift,
    time_inproj,
    time_bias,
    time_outproj,
    time_outbias,
    feed_gain,
    feed_shift,
    up_weight,
    up_bias,
    down_weight,
    down_bias,
    cotangent,
):
    clips_local = min(TIMES, lax.axis_size("dp"))
    times_local = TIMES // clips_local
    own_rows = tokens.shape[0] * tokens.shape[1]
    contract_rows = (((0,), (0,)), ((), ()))
    contract_cols = (((1,), (1,)), ((), ()))
    time_set = (time_inproj, time_bias, time_outproj)
    space_set = (space_inproj, space_bias, space_outproj)
    resid = tokens.reshape(own_rows, -1).astype(jnp.float32)
    after_space, space_kept = attention_forward(
        resid, space_gain, space_shift, space_set, space_outbias, False, times_local
    )
    after_time, time_kept = attention_forward(
        after_space, time_gain, time_shift, time_set, time_outbias, True, times_local
    )
    feed_normed, feed_pull = jax.vjp(layer_norm, after_time, feed_gain, feed_shift)
    feed_low = feed_normed.astype(jnp.bfloat16)
    branch_low = cotangent.reshape(own_rows, -1)
    upstream = branch_low.astype(jnp.float32)
    down_bias_grad = jnp.sum(branch_low, axis=0, dtype=jnp.float32)
    feed_full = full_rows(feed_low)
    pre_act = lax.dot_general(
        feed_full, up_weight, contract_cols, preferred_element_type=jnp.float32
    ) + up_bias.astype(jnp.float32)
    hidden = gelu_exact(pre_act).astype(jnp.bfloat16)

    def down_term(start, count):
        return jnp.dot(hidden, down_weight, preferred_element_type=jnp.float32)

    layer_sum = after_time + partial_rows(down_term, own_rows) + down_bias.astype(jnp.float32)
    branch_full = full_rows(branch_low)
    down_grad = lax.dot_general(
        hidden, branch_full, contract_rows, preferred_element_type=jnp.float32
    )
    hidden_grad = lax.dot_general(
        branch_full, down_weight, contract_cols, preferred_element_type=jnp.float32
    )
    pre_grad = (hidden_grad * gelu_slope(pre_act)).astype(jnp.bfloat16)
    up_grad = lax.dot_general(
        pre_grad, feed_full, contract_rows, preferred_element_type=jnp.float32
    )
    up_bias_grad = jnp.sum(pre_grad, axis=0, dtype=jnp.float32)

    def up_term(start, count):
        return jnp.dot(pre_grad, up_weight, preferred_element_type=jnp.float32)

    feed_grad = partial_rows(up_term, own_rows)
    resid_part, feed_gain_grad, feed_shift_grad = feed_pull(feed_grad)
    time_upstream = upstream + resid_part
    space_upstream, time_grads = attention_backward(
        time_upstream, time_kept, time_set, True, times_local
    )
    input_grad, space_grads = attention_backward(
        space_upstream, space_kept, space_set, False, times_local
    )
    summed = lax.psum(
        (
            space_grads[2],
            space_grads[3],
            space_grads[4],
            time_grads[2],
            time_grads[3],
            time_grads[4],
            up_grad,
            up_bias_grad,
            down_grad,
        ),
        "dp",
    )
    shared = lax.psum(
        (
            space_grads[0],
            space_grads[1],
            space_grads[5],
            time_grads[0],
            time_grads[1],
            time_grads[5],
            feed_gain_grad,
            feed_shift_grad,
            down_bias_grad,
        ),
        ("dp", "tensor"),
    )
    shape_out = tokens.shape
    return (
        layer_sum.astype(jnp.bfloat16).reshape(shape_out),
        input_grad.reshape(shape_out),
        shared[0],
        shared[1],
        summed[0],
        summed[1],
        summed[2],
        shared[2],
        shared[3],
        shared[4],
        summed[3],
        summed[4],
        summed[5],
        shared[5],
        shared[6],
        shared[7],
        summed[6],
        summed[7],
        summed[8],
        shared[8],
    )


def solution(mesh):
    return jax.shard_map(
        per_device,
        mesh=mesh,
        in_specs=(
            P(("dp", "tensor"), None, None),
            P(),
            P(),
            P(None, None, "tensor"),
            P(None, "tensor"),
            P("tensor", None),
            P(),
            P(),
            P(),
            P(None, None, "tensor"),
            P(None, "tensor"),
            P("tensor", None),
            P(),
            P(),
            P(),
            P("tensor", None),
            P("tensor"),
            P("tensor", None),
            P(),
            P(("dp", "tensor"), None, None),
        ),
        out_specs=(
            P(("dp", "tensor"), None, None),
            P(("dp", "tensor"), None, None),
            P(),
            P(),
            P(None, None, "tensor"),
            P(None, "tensor"),
            P("tensor", None),
            P(),
            P(),
            P(),
            P(None, None, "tensor"),
            P(None, "tensor"),
            P("tensor", None),
            P(),
            P(),
            P(),
            P("tensor", None),
            P("tensor"),
            P("tensor", None),
            P(),
        ),
        check_vma=False,
    )
```

profile of v0, /device:TPU:0, one launch (start us, length us, event | category | flops | bytes accessed | tf_op | source)
XLA Modules:
  0.0 2199.9 jit_solution(4943705803411020907)
XLA Ops:
  19.9 93.2 %all-gather.7.cloned.1.call-done = bf16[3136,768]{1,0:T(8,128)(2,1)} async-done(((bf16[784,768]{1,0:T(8,128)(2,1)}), bf16[3136,768]{1,0:T(8,128)(2,1)}) %all-gather.7.cloned.1.call-update) | async-done | bytes 4816912 | tf_op jit(solution)/shard_map/all_gather | solution.py:99
  113.1 7.1 add_convert_fusion.1
  120.2 15.5 reshape.274
  154.1 5.1 fusion.76
  160.0 162.2 %reduce-scatter.7.cloned.1.call-done = f32[784,768]{1,0:T(8,128)} async-done(((f32[3136,768]{1,0:T(8,128)}), f32[784,768]{1,0:T(8,128)}) %reduce-scatter.7.cloned.1.call-update) | async-done | bytes 2408464 | tf_op jit(solution)/shard_map/reduce_scatter | solution.py:103
  328.0 92.1 %all-gather.9.cloned.1.call-done = bf16[3136,768]{1,0:T(8,128)(2,1)} async-done(((bf16[784,768]{1,0:T(8,128)(2,1)}), bf16[3136,768]{1,0:T(8,128)(2,1)}) %all-gather.9.cloned.1.call-update) | async-done | bytes 4816912 | tf_op jit(solution)/shard_map/all_gather | solution.py:99
  420.1 7.1 add_convert_fusion
  427.1 9.2 reshape.277
  436.3 16.3 copy.164
  452.6 51.6 %all_to_all.60 = bf16[2,1568,576]{2,0,1:T(2,128)(2,1)} all-to-all(bf16[2,1568,576]{2,0,1:T(2,128)(2,1)} %copy.164), channel_id=1, replica_groups=mesh['dp'=8,'tensor'=4] {'dp'}, dimensions={1} | all-to-all | bytes 7225344 | tf_op jit(solution)/shard_map/all_to_all | solution.py:114
  504.2 13.3 copy.199
  548.7 23.4 %all_to_all.61 = bf16[16,196,192]{1,2,0:T(8,128)(2,1)S(1)} all-to-all(bf16[16,196,192]{1,2,0:T(8,128)(2,1)S(1)} %bitcast.180), channel_id=1, replica_groups=mesh['dp'=8,'tensor'=4] {'dp'}, dimensions={0} | all-to-all | bytes 2408448 | tf_op jit(solution)/shard_map/all_to_all | solution.py:121
  583.4 160.4 %reduce-scatter.9.cloned.1.call-done = f32[784,768]{1,0:T(8,128)} async-done(((f32[3136,768]{1,0:T(8,128)}), f32[784,768]{1,0:T(8,128)}) %reduce-scatter.9.cloned.1.call-update) | async-done | bytes 2408464 | tf_op jit(solution)/shard_map/reduce_scatter | solution.py:103
  752.2 89.5 %all-gather.11.cloned.1.call-done = bf16[3136,768]{1,0:T(8,128)(2,1)} async-done(((bf16[784,768]{1,0:T(8,128)(2,1)}), bf16[3136,768]{1,0:T(8,128)(2,1)}) %all-gather.11.cloned.1.call-update) | async-done | bytes 4816912 | tf_op jit(solution)/shard_map/all_gather | solution.py:99
  841.7 9.5 multiply_convert_fusion.1
  851.2 81.9 %all-gather.13.cloned.1.call-done = bf16[3136,768]{1,0:T(8,128)(2,1)} async-done(((bf16[784,768]{1,0:T(8,128)(2,1)}), bf16[3136,768]{1,0:T(8,128)(2,1)}) %all-gather.13.cloned.1.call-update) | async-done | bytes 4816912 | tf_op jit(solution)/shard_map/all_gather | solution.py:99
  933.1 9.9 convert_reduce_fusion
  945.1 6.3 fusion.79
  951.5 8.8 fusion.78
  961.0 153.3 %reduce-scatter.13.cloned.1.call-done = f32[784,768]{1,0:T(8,128)} async-done(((f32[3136,768]{1,0:T(8,128)}), f32[784,768]{1,0:T(8,128)}) %reduce-scatter.13.cloned.1.call-update) | async-done | bytes 2408464 | tf_op jit(solution)/shard_map/reduce_scatter | solution.py:103
  1117.7 164.4 %reduce-scatter.11.cloned.1.call-done = f32[784,768]{1,0:T(8,128)} async-done(((f32[3136,768]{1,0:T(8,128)}), f32[784,768]{1,0:T(8,128)}) %reduce-scatter.11.cloned.1.call-update) | async-done | bytes 2408464 | tf_op jit(solution)/shard_map/reduce_scatter | solution.py:103
  1282.0 5.2 fusion.69
  1289.1 92.2 %all-gather.15.cloned.1.call-done = bf16[3136,768]{1,0:T(8,128)(2,1)} async-done(((bf16[784,768]{1,0:T(8,128)(2,1)}), bf16[3136,768]{1,0:T(8,128)(2,1)}) %all-gather.15.cloned.1.call-update) | async-done | bytes 4816912 | tf_op jit(solution)/shard_map/all_gather | solution.py:99
  1390.4 7.2 copy.174
  1402.1 21.2 all-to-all-done.2
  1423.2 6.0 copy.201
  1450.5 10.7 copy.180
  1461.2 7.4 copy.181
  1468.6 51.8 %all_to_all.62 = bf16[16,196,576]{2,1,0:T(8,128)(2,1)S(1)} all-to-all(bf16[16,196,576]{2,1,0:T(8,128)(2,1)} %copy.181), channel_id=1, replica_groups=mesh['dp'=8,'tensor'=4] {'dp'}, dimensions={0} | all-to-all | bytes 7225344 | tf_op jit(solution)/shard_map/all_to_all | solution.py:121
  1524.7 5.4 reshape.285
  1530.1 10.0 fusion.80
  1540.1 161.0 %reduce-scatter.15.cloned.1.call-done = f32[784,768]{1,0:T(8,128)} async-done(((f32[3136,768]{1,0:T(8,128)}), f32[784,768]{1,0:T(8,128)}) %reduce-scatter.15.cloned.1.call-update) | async-done | bytes 2408464 | tf_op jit(solution)/shard_map/reduce_scatter | solution.py:103
  1709.3 92.1 %all-gather.17.cloned.1.call-done = bf16[3136,768]{1,0:T(8,128)(2,1)} async-done(((bf16[784,768]{1,0:T(8,128)(2,1)}), bf16[3136,768]{1,0:T(8,128)(2,1)}) %all-gather.17.cloned.1.call-update) | async-done | bytes 4816912 | tf_op jit(solution)/shard_map/all_gather | solution.py:99
  1806.5 7.1 reshape.286
  1813.6 7.8 fusion.46
  1821.4 8.8 multiply_reduce_fusion
  1830.2 11.1 multiply_convert_fusion
  1854.0 10.0 convert_element_type.196
  1863.9 9.9 fusion.81
  1874.2 9.6 fusion.85
  1883.8 9.6 fusion.84
  1895.4 6.5 copy.189
  1901.8 7.9 fusion.13
  1914.3 6.7 fusion.15
  1931.0 15.5 all-reduce.1
  1946.5 90.2 %reduce-scatter.17.cloned.1.call-done = f32[784,768]{1,0:T(8,128)} async-done(((f32[3136,768]{1,0:T(8,128)}), f32[784,768]{1,0:T(8,128)}) %reduce-scatter.17.cloned.1.call-update) | async-done | bytes 2408464 | tf_op jit(solution)/shard_map/reduce_scatter | solution.py:103
  2052.2 43.8 %all-reduce = (f32[768]{0:T(1024)}, f32[768]{0:T(1024)}, f32[768]{0:T(1024)}, f32[768]{0:T(1024)}, f32[768]{0:T(1024)}, /*index=5*/f32[768]{0:T(1024)}, f32[768]{0:T(1024)}, f32[768]{0:T(1024)}, f32[768]{0:T(1024)}) all-reduce(f32[768]{0:T(1024)S(1)} %get-tuple-element.124, ...), channel_id=1, replica_groups=mesh['dp'=8,'tensor'=4] {'dp','tensor'}, use_global_device_ids=true, to_apply=%region_25.0 | all-reduce | flops 6912 | bytes 55296 | tf_op jit(solution)/shard_map/psum | solution.py:319
  2096.0 86.8 %all-reduce.5.cloned.1.call-done = (f32[768,3,192]{0,2,1:T(8,128)}, f32[192,768]{1,0:T(8,128)}, f32[768,3,192]{0,2,1:T(8,128)}, f32[192,768]{1,0:T(8,128)}, f32[768,768]{1,0:T(8,128)}, /*index=5*/f32[768,768]{1,0:T(8,128)}) async-done(((f32[768,3,192]{0,2,1:T(8,128)}, f32[192,768]{1,0:T(8,128)}, f32[768,3,192]{0,2,1:T(8,128)}, f32[192,768]{1,0:T(8,128)}, f32[768,768]{1,0:T(8,128)}, ...) | async-done | bytes 9437200 | tf_op jit(solution)/shard_map/psum | solution.py:305
  (288 shorter events, 203.8 us)
Async XLA Ops:
  7.2 834.5 %copy-start = (bf16[768,768]{1,0:T(8,128)(2,1)S(1)}, bf16[768,768]{1,0:T(8,128)(2,1)}, u32[]{:S(2)}) copy-start(bf16[768,768]{1,0:T(8,128)(2,1)} %param.35) | copy-start | bytes 3538948
  7.2 105.9 %all-gather.7.cloned.1.call-start = ((), (), s32[]{:S(2)}) async-start(), calls=%async_computation.10 | async-start | bytes 6021120 | tf_op jit(solution)/shard_map/all_gather | solution.py:99
  15.9 3.9 copy-start.67
  15.9 97.2 %copy-start.74 = (bf16[768,3,192]{0,2,1:T(8,128)(2,1)S(1)}, bf16[768,3,192]{0,2,1:T(8,128)(2,1)}, u32[]{:S(2)}) copy-start(bf16[768,3,192]{0,2,1:T(8,128)(2,1)} %param.23) | copy-start | bytes 2654212
  19.2 303.0 %reduce-scatter.7.cloned.1.call-start = ((), (), s32[]{:S(2)}) async-start(), calls=%async_computation.11 | async-start | bytes 12042240 | tf_op jit(solution)/shard_map/reduce_scatter | solution.py:103
  138.3 5.5 copy-start.31
  143.8 4.6 copy-start.48
  148.5 5.7 copy-start.46
  154.1 5.2 copy-start.27
  159.3 260.8 %all-gather.9.cloned.1.call-start = ((), (), s32[]{:S(2)}) async-start(), calls=%async_computation.12 | async-start | bytes 6021120 | tf_op jit(solution)/shard_map/all_gather | solution.py:99
  326.4 93.7 %copy-start.73 = (bf16[768,3,192]{0,2,1:T(8,128)(2,1)S(1)}, bf16[768,3,192]{0,2,1:T(8,128)(2,1)}, u32[]{:S(2)}) copy-start(bf16[768,3,192]{0,2,1:T(8,128)(2,1)} %param.29) | copy-start | bytes 2654212
  327.9 415.9 %reduce-scatter.9.cloned.1.call-start = ((), (), s32[]{:S(2)}) async-start(), calls=%async_computation.13 | async-start | bytes 12042240 | tf_op jit(solution)/shard_map/reduce_scatter | solution.py:103
  572.1 5.5 copy-start.44
  577.5 5.2 copy-start.29
  582.7 259.0 %all-gather.11.cloned.1.call-start = ((), (), s32[]{:S(2)}) async-start(), calls=%async_computation.14 | async-start | bytes 6021120 | tf_op jit(solution)/shard_map/all_gather | solution.py:99
  749.5 183.6 %all-gather.13.cloned.1.call-start = ((), (), s32[]{:S(2)}) async-start(), calls=%async_computation.16 | async-start | bytes 6021120 | tf_op jit(solution)/shard_map/all_gather | solution.py:99
  752.1 362.2 %reduce-scatter.13.cloned.1.call-start = ((), (), s32[]{:S(2)}) async-start(), calls=%async_computation.17 | async-start | bytes 12042240 | tf_op jit(solution)/shard_map/reduce_scatter | solution.py:103
  752.2 180.9 %copy-start.72 = (bf16[768,768]{1,0:T(8,128)(2,1)S(1)}, bf16[768,768]{1,0:T(8,128)(2,1)}, u32[]{:S(2)}) copy-start(bf16[768,768]{1,0:T(8,128)(2,1)} %param.37) | copy-start | bytes 3538948
  951.5 330.6 %reduce-scatter.11.cloned.1.call-start = ((), (), s32[]{:S(2)}) async-start(), calls=%async_computation.15 | async-start | bytes 12042240 | tf_op jit(solution)/shard_map/reduce_scatter | solution.py:103
  960.3 420.9 %all-gather.15.cloned.1.call-start = ((), (), s32[]{:S(2)}) async-start(), calls=%async_computation.18 | async-start | bytes 6021120 | tf_op jit(solution)/shard_map/all_gather | solution.py:99
  1117.6 169.6 %copy-start.12 = (bf16[784,768]{1,0:T(8,128)(2,1)S(1)}, bf16[784,768]{1,0:T(8,128)(2,1)}, u32[]{:S(2)}) copy-start(bf16[784,768]{1,0:T(8,128)(2,1)} %reshape.282) | copy-start | bytes 3612676
  1287.2 94.0 %copy-start.45 = (bf16[192,768]{1,0:T(8,128)(2,1)S(1)}, bf16[192,768]{1,0:T(8,128)(2,1)}, u32[]{:S(2)}) copy-start(bf16[192,768]{1,0:T(8,128)(2,1)} %param.31) | copy-start | bytes 884740
  1390.4 11.5 copy-start.39
  1397.6 25.7 %all-to-all-start.2 = ((bf16[2,1568,192]{2,0,1:T(2,128)(2,1)}), bf16[2,1568,192]{2,0,1:T(2,128)(2,1)}, u32[]{:S(2)}, u32[]{:S(2)}) async-start(bf16[2,1568,192]{2,0,1:T(2,128)(2,1)} %copy.174), calls=%async_computation.6 | async-start | bytes 3211264 | tf_op jit(solution)/shard_map/all_to_all | solution.py:114
  1401.8 299.3 %reduce-scatter.15.cloned.1.call-start = ((), (), s32[]{:S(2)}) async-start(), calls=%async_computation.19 | async-start | bytes 12042240 | tf_op jit(solution)/shard_map/reduce_scatter | solution.py:103
  1429.2 9.5 slice-start
  1434.0 4.7 slice-start.1
  1434.0 5.1 copy-start.19
  1434.0 5.8 copy-start.26
  1540.1 164.5 %copy-start.59 = (f32[784]{0:T(1024)S(1)}, f32[784]{0:T(1024)}, u32[]{:S(2)}) copy-start(f32[784]{0:T(1024)} %copy-done.58) | copy-start | bytes 9412
  1540.1 261.3 %all-gather.17.cloned.1.call-start = ((), (), s32[]{:S(2)}) async-start(), calls=%async_computation.20 | async-start | bytes 6021120 | tf_op jit(solution)/shard_map/all_gather | solution.py:99
  1707.4 94.0 %copy-start.47 = (bf16[192,768]{1,0:T(8,128)(2,1)S(1)}, bf16[192,768]{1,0:T(8,128)(2,1)}, u32[]{:S(2)}) copy-start(bf16[192,768]{1,0:T(8,128)(2,1)} %param.25) | copy-start | bytes 884740
  1709.2 327.6 %reduce-scatter.17.cloned.1.call-start = ((), (), s32[]{:S(2)}) async-start(), calls=%async_computation.21 | async-start | bytes 12042240 | tf_op jit(solution)/shard_map/reduce_scatter | solution.py:103
  1813.6 7.8 copy-start.20
  1813.6 7.8 copy-start.32
  1841.2 4.5 copy-start.5
  1841.2 4.8 copy-start.14
  1873.9 308.9 %all-reduce.5.cloned.1.call-start = ((), (), s32[]{:S(2)}) async-start(), calls=%async_computation.22 | async-start | bytes 18874368 | tf_op jit(solution)/shard_map/psum | solution.py:305
  1874.2 19.2 slice-start.2
  1883.8 9.6 copy-start.30
  1883.8 9.6 slice-start.3
  1901.8 7.9 copy-start.28
  1909.8 4.6 copy-start.34
  1927.9 108.9 %copy-start.51 = (f32[784]{0:T(1024)S(1)}, f32[784]{0:T(1024)}, u32[]{:S(2)}) copy-start(f32[784]{0:T(1024)} %copy-done.50) | copy-start | bytes 9412
  1927.9 108.9 %copy-start.53 = (f32[784]{0:T(1024)S(1)}, f32[784]{0:T(1024)}, u32[]{:S(2)}) copy-start(f32[784]{0:T(1024)} %copy-done.52) | copy-start | bytes 9412
  1927.9 108.9 %copy-start.57 = (f32[768]{0:T(1024)S(1)}, f32[768]{0:T(1024)}, u32[]{:S(2)}) copy-start(f32[768]{0:T(1024)} %param.21) | copy-start | bytes 9220
  1946.5 93.8 %copy-start.61 = (f32[784]{0:T(1024)S(1)}, f32[784]{0:T(1024)}, u32[]{:S(2)}) copy-start(f32[784]{0:T(1024)} %copy-done.60) | copy-start | bytes 9412
  2189.1 3.9 copy-start.1
  (46 other events, 105.5 us)
Sparse Core Ops, SparseCore 0:
  19.3 93.7 all-gather.6
  159.4 162.6 reduce-scatter.6
  328.0 92.0 all-gather.8
  582.8 160.8 reduce-scatter.8
  749.6 92.0 all-gather.10
  843.7 89.3 all-gather.12
  951.6 162.6 reduce-scatter.12
  1116.7 165.3 reduce-scatter.10
  1289.2 92.0 all-gather.14
  1540.2 160.8 reduce-scatter.14
  1709.3 92.0 all-gather.16
  1874.0 162.6 reduce-scatter.16
  2043.0 139.7 all-reduce.4
where the time goes:
time: 2210 us; the launch traced here: 2200 us
  waiting for transfers between devices  1540 us (70%)
  local copies, waits for them, and re-layouts  211 us (10%)
  blocking collectives  186 us (8%)
  matrix products  174 us (8%)
  other arithmetic  67.5 us (3%)
    reduce_scatter x6, waiting for transfers between devices, partial_rows(): lax.psum_scatter(make_term(jnp.int32(0), own_rows * lax.axis_size('tensor...  891 us
    all_gather x6, waiting for transfers between devices, full_rows(): return lax.all_gather(shard, 'tensor', axis=0, tiled=True)  541 us
    psum x1, waiting for transfers between devices, per_device(): lax.psum((space_grads[2], space_grads[3], space_grads[4], time_grads[2],...  86.8 us
    all_to_all x2, blocking collectives, to_frames(): lax.all_to_all(grouped, 'dp', split_axis=0, concat_axis=1, tiled=True)  75.2 us
    all_to_all x1, blocking collectives, to_patches(): lax.all_to_all(grouped, 'dp', split_axis=1, concat_axis=0, tiled=True)  51.6 us
    unnamed x174, local copies, waits for them, and re-layouts  46.9 us
  transfers between devices with their start and end apart: 14, of which 14 were waited for; matrix products, arithmetic and copies ran while one was open for 4% of the time, Pallas kernels for 0%

commit v1 on v0

--- a/solution.py
+++ b/solution.py
@@ -1,3 +1,4 @@
+import functools
 import jax
 import jax.numpy as jnp
 from jax import lax
@@ -9,6 +10,37 @@
 EPSILON = 1e-06
 ROOT_HALF = 0.7071067811865476
 INV_ROOT_TAU = 0.3989422804014327
+
+
+def lift_members_all(xin, array_axis):
+    xin = jnp.moveaxis(xin, 0, array_axis)
+    row_out = xin.shape
+    return xin.reshape(
+        *row_out[:array_axis],
+        row_out[array_axis] * row_out[array_axis + 1],
+        *row_out[array_axis + 2 :]
+    )
+
+
+def load_units(packet, comm_axis, which_dim):
+    full_n = lax.axis_size(comm_axis)
+    found = tuple(((num, (num + 1) % full_n) for num in range(full_n)))
+    all_rows = tuple(((u, s) for s, u in found))
+    big, part_next = ([], [])
+    for i in range(full_n - 1):
+        if i % 2 == 0:
+            big.append(lax.ppermute(big[-1] if big else packet, comm_axis, found))
+        else:
+            part_next.append(
+                lax.ppermute(part_next[-1] if part_next else packet, comm_axis, all_rows)
+            )
+    mid_arr = jnp.stack([*big[::-1], packet, *part_next], 0)
+    local_out = lax.axis_index(comm_axis) - len(big)
+    mid_arr = mid_arr[(jnp.arange(full_n) - local_out) % full_n]
+    return lift_members_all(mid_arr, which_dim)
+
+
+connect_lanes_up = functools.partial(load_units, comm_axis="tensor", which_dim=0)
 
 
 def layer_norm(values, gain, shift):
@@ -96,7 +128,7 @@
 
 
 def full_rows(shard):
-    return lax.all_gather(shard, "tensor", axis=0, tiled=True)
+    return connect_lanes_up(shard)
 
 
 def partial_rows(make_term, own_rows):

time: 2210 us -> 2190 us (level)
  waiting for transfers between devices: 1540 us -> 1340 us
  starting transfers between devices: 6.14 us -> 131 us
  local copies, waits for them, and re-layouts: 211 us -> 251 us
  other arithmetic: 67.5 us -> 92.4 us
    all_gather x6 -> x0, waiting for transfers between devices: 541 us -> none  [full_rows(): return lax.all_gather(shard, 'tensor', axis=0, tiled=True)]
    ppermute x0 -> x18, waiting for transfers between devices: none -> 314 us  [the longest x12 282 us: load_units(): big.append(lax.ppermute(big[-1] if big else packet, comm_axis, found))]
    ppermute x0 -> x18, starting transfers between devices: none -> 127 us  [the longest x12 111 us: load_units(): big.append(lax.ppermute(big[-1] if big else packet, comm_axis, found))]
    gather x0 -> x6, local copies, waits for them, and re-layouts: none -> 32.8 us  [load_units(): mid_arr = mid_arr[(jnp.arange(full_n) - local_out) % full_n]]
    reduce_scatter x6, waiting for transfers between devices: 891 us -> 919 us  [partial_rows(): lax.psum_scatter(make_term(jnp.int32(0), own_rows * lax.axis_size('tensor...]
    another operation x0 -> x8, other arithmetic: none -> 26.1 us  [load_units(): mid_arr = jnp.stack([*big[::-1], packet, *part_next], 0)]
    unnamed x174 -> x200, local copies, waits for them, and re-layouts: 46.9 us -> 48.6 us
  transfers between devices with their start and end apart: 14 -> 26, of which waited for: 14 -> 24; matrix products, arithmetic and copies ran while one was open for 4% -> 5% of each run, Pallas kernels for 0% -> 0%
where the time goes in v1:
time: 2190 us; the launch traced here: 2180 us
  waiting for transfers between devices  1340 us (61%)
  local copies, waits for them, and re-layouts  251 us (11%)
  blocking collectives  185 us (8%)
  matrix products  168 us (8%)
  starting transfers between devices  131 us (6%)
  other arithmetic  92.4 us (4%)
    reduce_scatter x6, waiting for transfers between devices, partial_rows(): lax.psum_scatter(make_term(jnp.int32(0), own_rows * lax.axis_size('tensor...  919 us
    ppermute x12, waiting for transfers between devices, load_units(): big.append(lax.ppermute(big[-1] if big else packet, comm_axis, found))  282 us
    ppermute x12, starting transfers between devices, load_units(): big.append(lax.ppermute(big[-1] if big else packet, comm_axis, found))  111 us
    psum x1, waiting for transfers between devices, per_device(): lax.psum((space_grads[2], space_grads[3], space_grads[4], time_grads[2],...  86.7 us
    all_to_all x2, blocking collectives, to_frames(): lax.all_to_all(grouped, 'dp', split_axis=0, concat_axis=1, tiled=True)  75.2 us
    all_to_all x1, blocking collectives, to_patches(): lax.all_to_all(grouped, 'dp', split_axis=1, concat_axis=0, tiled=True)  51.8 us
    unnamed x200, local copies, waits for them, and re-layouts  48.6 us
  transfers between devices with their start and end apart: 26, of which 24 were waited for; matrix products, arithmetic and copies ran while one was open for 5% of the time, Pallas kernels for 0%

profile of v1, /device:TPU:0, one launch (start us, length us, event | category | flops | bytes accessed | tf_op | source)
XLA Modules:
  0.0 2183.6 jit_solution(6206216354318372349)
XLA Ops:
  23.2 27.4 %collective-permute-done = bf16[784,768]{1,0:T(8,128)(2,1)} collective-permute-done((bf16[784,768]{1,0:T(8,128)(2,1)S(1)}, bf16[784,768]{1,0:T(8,128)(2,1)}, u32[]{:S(2)}, u32[]{:S(2)}) %collective-permute-start) | collective-permute-done | bytes 1204256 | tf_op jit(solution)/shard_map/ppermute | solution.py:32
  56.4 18.8 collective-permute-done.2
  75.2 26.2 %collective-permute-done.1 = bf16[784,768]{1,0:T(8,128)(2,1)} collective-permute-done((bf16[784,768]{1,0:T(8,128)(2,1)}, bf16[784,768]{1,0:T(8,128)(2,1)}, u32[]{:S(2)}, u32[]{:S(2)}) %collective-permute-start.1) | collective-permute-done | bytes 1204256 | tf_op jit(solution)/shard_map/ppermute | solution.py:32
  119.2 15.5 reshape.447
  159.0 163.1 %reduce-scatter.7.cloned.1.call-done = f32[784,768]{1,0:T(8,128)} async-done(((f32[3136,768]{1,0:T(8,128)}), f32[784,768]{1,0:T(8,128)}) %reduce-scatter.7.cloned.1.call-update) | async-done | bytes 2408464 | tf_op jit(solution)/shard_map/reduce_scatter | solution.py:135
  330.0 27.4 %collective-permute-done.3 = bf16[784,768]{1,0:T(8,128)(2,1)S(1)} collective-permute-done((bf16[784,768]{1,0:T(8,128)(2,1)S(1)}, bf16[784,768]{1,0:T(8,128)(2,1)S(1)}, u32[]{:S(2)}, u32[]{:S(2)}) %collective-permute-start.3) | collective-permute-done | bytes 1204256 | tf_op jit(solution)/shard_map/ppermute | solution.py:32
  357.4 25.1 %collective-permute-start.4 = (bf16[784,768]{1,0:T(8,128)(2,1)S(1)}, bf16[784,768]{1,0:T(8,128)(2,1)S(1)}, u32[]{:S(2)}, u32[]{:S(2)}) collective-permute-start(bf16[784,768]{1,0:T(8,128)(2,1)S(1)} %collective-permute-done.3), channel_id=1, source_target_pairs={{0,1},{1,2},{2,3},{3,0},{4,5},{5,6},{6,7},{7,4},{8,9},{9,10},{10,1... | collective-permute-start | bytes 3612680 | tf_op jit(solution)/shard_map/ppermute | solution.py:32
  383.1 24.5 %collective-permute-done.4 = bf16[784,768]{1,0:T(8,128)(2,1)S(1)} collective-permute-done((bf16[784,768]{1,0:T(8,128)(2,1)S(1)}, bf16[784,768]{1,0:T(8,128)(2,1)S(1)}, u32[]{:S(2)}, u32[]{:S(2)}) %collective-permute-start.4) | collective-permute-done | bytes 1204256 | tf_op jit(solution)/shard_map/ppermute | solution.py:32
  422.7 9.2 reshape.451
  431.8 16.3 copy.173
  448.2 51.8 %all_to_all.60 = bf16[2,1568,576]{2,0,1:T(2,128)(2,1)} all-to-all(bf16[2,1568,576]{2,0,1:T(2,128)(2,1)} %copy.173), channel_id=1, replica_groups=mesh['dp'=8,'tensor'=4] {'dp'}, dimensions={1} | all-to-all | bytes 7225344 | tf_op jit(solution)/shard_map/all_to_all | solution.py:146
  500.0 13.3 copy.209
  544.5 23.4 %all_to_all.61 = bf16[16,196,192]{1,2,0:T(8,128)(2,1)S(1)} all-to-all(bf16[16,196,192]{1,2,0:T(8,128)(2,1)S(1)} %bitcast.212), channel_id=1, replica_groups=mesh['dp'=8,'tensor'=4] {'dp'}, dimensions={0} | all-to-all | bytes 2408448 | tf_op jit(solution)/shard_map/all_to_all | solution.py:153
  582.9 183.5 %reduce-scatter.9.cloned.1.call-done = f32[784,768]{1,0:T(8,128)} async-done(((f32[3136,768]{1,0:T(8,128)}), f32[784,768]{1,0:T(8,128)}) %reduce-scatter.9.cloned.1.call-update) | async-done | bytes 2408464 | tf_op jit(solution)/shard_map/reduce_scatter | solution.py:135
  779.0 23.9 %collective-permute-done.6 = bf16[784,768]{1,0:T(8,128)(2,1)} collective-permute-done((bf16[784,768]{1,0:T(8,128)(2,1)}, bf16[784,768]{1,0:T(8,128)(2,1)}, u32[]{:S(2)}, u32[]{:S(2)}) %collective-permute-start.6) | collective-permute-done | bytes 1204256 | tf_op jit(solution)/shard_map/ppermute | solution.py:32
  802.9 25.3 %collective-permute-start.7 = (bf16[784,768]{1,0:T(8,128)(2,1)}, bf16[784,768]{1,0:T(8,128)(2,1)}, u32[]{:S(2)}, u32[]{:S(2)}) collective-permute-start(bf16[784,768]{1,0:T(8,128)(2,1)} %collective-permute-done.6), channel_id=1, source_target_pairs={{0,1},{1,2},{2,3},{3,0},{4,5},{5,6},{6,7},{7,4},{8,9},{9,10},{10,1... | collective-permute-start | bytes 3612680 | tf_op jit(solution)/shard_map/ppermute | solution.py:32
  830.4 24.1 %collective-permute-done.10 = bf16[784,768]{1,0:T(8,128)(2,1)} collective-permute-done((bf16[784,768]{1,0:T(8,128)(2,1)}, bf16[784,768]{1,0:T(8,128)(2,1)}, u32[]{:S(2)}, u32[]{:S(2)}) %collective-permute-start.10) | collective-permute-done | bytes 1204256 | tf_op jit(solution)/shard_map/ppermute | solution.py:32
  867.7 12.5 collective-permute-done.8
  880.2 24.6 %collective-permute-done.7 = bf16[784,768]{1,0:T(8,128)(2,1)} collective-permute-done((bf16[784,768]{1,0:T(8,128)(2,1)}, bf16[784,768]{1,0:T(8,128)(2,1)}, u32[]{:S(2)}, u32[]{:S(2)}) %collective-permute-start.7) | collective-permute-done | bytes 1204256 | tf_op jit(solution)/shard_map/ppermute | solution.py:32
  915.5 8.1 multiply_convert_fusion.1
  923.6 7.8 convert_reduce_fusion
  941.2 8.7 fusion.76
  950.6 152.3 %reduce-scatter.13.cloned.1.call-done = f32[784,768]{1,0:T(8,128)} async-done(((f32[3136,768]{1,0:T(8,128)}), f32[784,768]{1,0:T(8,128)}) %reduce-scatter.13.cloned.1.call-update) | async-done | bytes 2408464 | tf_op jit(solution)/shard_map/reduce_scatter | solution.py:135
  1106.8 163.6 %reduce-scatter.11.cloned.1.call-done = f32[784,768]{1,0:T(8,128)} async-done(((f32[3136,768]{1,0:T(8,128)}), f32[784,768]{1,0:T(8,128)}) %reduce-scatter.11.cloned.1.call-update) | async-done | bytes 2408464 | tf_op jit(solution)/shard_map/reduce_scatter | solution.py:135
  1281.1 27.2 %collective-permute-done.12 = bf16[784,768]{1,0:T(8,128)(2,1)S(1)} collective-permute-done((bf16[784,768]{1,0:T(8,128)(2,1)S(1)}, bf16[784,768]{1,0:T(8,128)(2,1)S(1)}, u32[]{:S(2)}, u32[]{:S(2)}) %collective-permute-start.12) | collective-permute-done | bytes 1204256 | tf_op jit(solution)/shard_map/ppermute | solution.py:32
  1308.3 25.3 %collective-permute-start.13 = (bf16[784,768]{1,0:T(8,128)(2,1)S(1)}, bf16[784,768]{1,0:T(8,128)(2,1)S(1)}, u32[]{:S(2)}, u32[]{:S(2)}) collective-permute-start(bf16[784,768]{1,0:T(8,128)(2,1)S(1)} %collective-permute-done.12), channel_id=1, source_target_pairs={{0,1},{1,2},{2,3},{3,0},{4,5},{5,6},{6,7},{7,4},{8,9},{9,10},{10,1... | collective-permute-start | bytes 3612680 | tf_op jit(solution)/shard_map/ppermute | solution.py:32
  1334.0 24.5 %collective-permute-done.13 = bf16[784,768]{1,0:T(8,128)(2,1)S(1)} collective-permute-done((bf16[784,768]{1,0:T(8,128)(2,1)S(1)}, bf16[784,768]{1,0:T(8,128)(2,1)S(1)}, u32[]{:S(2)}, u32[]{:S(2)}) %collective-permute-start.13) | collective-permute-done | bytes 1204256 | tf_op jit(solution)/shard_map/ppermute | solution.py:32
  1387.1 21.2 all-to-all-done.2
  1435.4 10.7 copy.190
  1446.1 7.4 copy.191
  1453.6 51.8 %all_to_all.62 = bf16[16,196,576]{2,1,0:T(8,128)(2,1)S(1)} all-to-all(bf16[16,196,576]{2,1,0:T(8,128)(2,1)} %copy.191), channel_id=1, replica_groups=mesh['dp'=8,'tensor'=4] {'dp'}, dimensions={0} | all-to-all | bytes 7225344 | tf_op jit(solution)/shard_map/all_to_all | solution.py:153
  1515.0 10.0 fusion.78
  1525.1 162.0 %reduce-scatter.15.cloned.1.call-done = f32[784,768]{1,0:T(8,128)} async-done(((f32[3136,768]{1,0:T(8,128)}), f32[784,768]{1,0:T(8,128)}) %reduce-scatter.15.cloned.1.call-update) | async-done | bytes 2408464 | tf_op jit(solution)/shard_map/reduce_scatter | solution.py:135
  1698.6 27.4 %collective-permute-done.15 = bf16[784,768]{1,0:T(8,128)(2,1)S(1)} collective-permute-done((bf16[784,768]{1,0:T(8,128)(2,1)S(1)}, bf16[784,768]{1,0:T(8,128)(2,1)S(1)}, u32[]{:S(2)}, u32[]{:S(2)}) %collective-permute-start.15) | collective-permute-done | bytes 1204256 | tf_op jit(solution)/shard_map/ppermute | solution.py:32
  1726.0 25.5 %collective-permute-start.16 = (bf16[784,768]{1,0:T(8,128)(2,1)S(1)}, bf16[784,768]{1,0:T(8,128)(2,1)S(1)}, u32[]{:S(2)}, u32[]{:S(2)}) collective-permute-start(bf16[784,768]{1,0:T(8,128)(2,1)S(1)} %collective-permute-done.15), channel_id=1, source_target_pairs={{0,1},{1,2},{2,3},{3,0},{4,5},{5,6},{6,7},{7,4},{8,9},{9,10},{10,1... | collective-permute-start | bytes 3612680 | tf_op jit(solution)/shard_map/ppermute | solution.py:32
  1751.7 24.5 %collective-permute-done.16 = bf16[784,768]{1,0:T(8,128)(2,1)S(1)} collective-permute-done((bf16[784,768]{1,0:T(8,128)(2,1)S(1)}, bf16[784,768]{1,0:T(8,128)(2,1)S(1)}, u32[]{:S(2)}, u32[]{:S(2)}) %collective-permute-start.16) | collective-permute-done | bytes 1204256 | tf_op jit(solution)/shard_map/ppermute | solution.py:32
  1796.0 7.8 fusion.42
  1803.8 9.0 multiply_reduce_fusion
  1812.7 11.2 multiply_convert_fusion
  1836.4 10.2 convert_element_type.220
  1846.6 9.8 fusion.79
  1856.5 9.6 fusion.85
  1866.1 9.6 fusion.84
  1884.4 8.1 fusion.82
  1911.4 13.9 all-reduce.1
  1925.3 95.0 %reduce-scatter.17.cloned.1.call-done = f32[784,768]{1,0:T(8,128)} async-done(((f32[3136,768]{1,0:T(8,128)}), f32[784,768]{1,0:T(8,128)}) %reduce-scatter.17.cloned.1.call-update) | async-done | bytes 2408464 | tf_op jit(solution)/shard_map/reduce_scatter | solution.py:135
  2036.0 43.7 %all-reduce = (f32[768]{0:T(1024)}, f32[768]{0:T(1024)}, f32[768]{0:T(1024)}, f32[768]{0:T(1024)}, f32[768]{0:T(1024)}, /*index=5*/f32[768]{0:T(1024)}, f32[768]{0:T(1024)}, f32[768]{0:T(1024)}, f32[768]{0:T(1024)}) all-reduce(f32[768]{0:T(1024)S(1)} %get-tuple-element.124, ...), channel_id=1, replica_groups=mesh['dp'=8,'tensor'=4] {'dp','tensor'}, use_global_device_ids=true, to_apply=%region_25.26 | all-reduce | flops 6912 | bytes 55296 | tf_op jit(solution)/shard_map/psum | solution.py:351
  2079.7 86.7 %all-reduce.5.cloned.1.call-done = (f32[768,3,192]{0,2,1:T(8,128)}, f32[192,768]{1,0:T(8,128)}, f32[768,3,192]{0,2,1:T(8,128)}, f32[192,768]{1,0:T(8,128)}, f32[768,768]{1,0:T(8,128)}, /*index=5*/f32[768,768]{1,0:T(8,128)}) async-done(((f32[768,3,192]{0,2,1:T(8,128)}, f32[192,768]{1,0:T(8,128)}, f32[768,3,192]{0,2,1:T(8,128)}, f32[192,768]{1,0:T(8,128)}, f32[768,768]{1,0:T(8,128)}, ...) | async-done | bytes 9437200 | tf_op jit(solution)/shard_map/psum | solution.py:337
  (353 shorter events, 360.1 us)
Async XLA Ops:
  7.2 908.3 %copy-start = (bf16[768,768]{1,0:T(8,128)(2,1)S(1)}, bf16[768,768]{1,0:T(8,128)(2,1)}, u32[]{:S(2)}) copy-start(bf16[768,768]{1,0:T(8,128)(2,1)} %param.35) | copy-start | bytes 3538948
  7.2 314.9 %reduce-scatter.7.cloned.1.call-start = ((), (), s32[]{:S(2)}) async-start(), calls=%async_computation.10 | async-start | bytes 12042240 | tf_op jit(solution)/shard_map/reduce_scatter | solution.py:135
  12.2 42.0 %copy-start.52 = (f32[784]{0:T(1024)}, f32[784]{0:T(1024)S(1)}, u32[]{:S(2)}) copy-start(f32[784]{0:T(1024)S(1)} %div.73) | copy-start | bytes 9412
  13.0 41.2 %copy-start.54 = (f32[784]{0:T(1024)}, f32[784]{0:T(1024)S(1)}, u32[]{:S(2)}) copy-start(f32[784]{0:T(1024)S(1)} %rsqrt.30) | copy-start | bytes 9412
  18.0 32.6 %collective-permute-start = (bf16[784,768]{1,0:T(8,128)(2,1)S(1)}, bf16[784,768]{1,0:T(8,128)(2,1)}, u32[]{:S(2)}, u32[]{:S(2)}) collective-permute-start(bf16[784,768]{1,0:T(8,128)(2,1)S(1)} %add_convert_fusion.6), channel_id=1, source_target_pairs={{0,1},{1,2},{2,3},{3,0},{4,5},{5,6},{6,7},{7,4},{8,9},{9,10},{10,1... | collective-permute-start | bytes 3612680 | tf_op jit(solution)/shard_map/ppermute | solution.py:32
  21.1 54.1 %collective-permute-start.2 = (bf16[784,768]{1,0:T(8,128)(2,1)S(1)}, bf16[784,768]{1,0:T(8,128)(2,1)}, u32[]{:S(2)}, u32[]{:S(2)}) collective-permute-start(bf16[784,768]{1,0:T(8,128)(2,1)S(1)} %add_convert_fusion.6), channel_id=1, source_target_pairs={{1,0},{2,1},{3,2},{0,3},{5,4},{6,5},{7,6},{4,7},{9,8},{10,9},{11,1... | collective-permute-start | bytes 3612680 | tf_op jit(solution)/shard_map/ppermute | solution.py:35
  50.6 50.8 %collective-permute-start.1 = (bf16[784,768]{1,0:T(8,128)(2,1)}, bf16[784,768]{1,0:T(8,128)(2,1)}, u32[]{:S(2)}, u32[]{:S(2)}) collective-permute-start(bf16[784,768]{1,0:T(8,128)(2,1)} %collective-permute-done), channel_id=1, source_target_pairs={{0,1},{1,2},{2,3},{3,0},{4,5},{5,6},{6,7},{7,4},{8,9},{9,10},{10,1... | collective-permute-start | bytes 3612680 | tf_op jit(solution)/shard_map/ppermute | solution.py:32
  158.3 608.1 %reduce-scatter.9.cloned.1.call-start = ((), (), s32[]{:S(2)}) async-start(), calls=%async_computation.11 | async-start | bytes 12042240 | tf_op jit(solution)/shard_map/reduce_scatter | solution.py:135
  324.9 57.6 %copy-start.4 = (f32[784,768]{1,0:T(8,128)}, f32[784,768]{1,0:T(8,128)S(1)}, u32[]{:S(2)}) copy-start(f32[784,768]{1,0:T(8,128)S(1)} %get-tuple-element.162) | copy-start | bytes 7225348
  324.9 57.5 %copy-start.50 = (f32[784]{0:T(1024)}, f32[784]{0:T(1024)S(1)}, u32[]{:S(2)}) copy-start(f32[784]{0:T(1024)S(1)} %broadcast_multiply_fusion.2) | copy-start | bytes 9412
  325.4 57.5 %copy-start.63 = (f32[784]{0:T(1024)}, f32[784]{0:T(1024)S(1)}, u32[]{:S(2)}) copy-start(f32[784]{0:T(1024)S(1)} %multiply_reduce_fusion.11) | copy-start | bytes 9412
  325.6 57.3 %copy-start.56 = (f32[784]{0:T(1024)}, f32[784]{0:T(1024)S(1)}, u32[]{:S(2)}) copy-start(f32[784]{0:T(1024)S(1)} %fusion.54) | copy-start | bytes 9412
  326.1 31.3 %collective-permute-start.3 = (bf16[784,768]{1,0:T(8,128)(2,1)S(1)}, bf16[784,768]{1,0:T(8,128)(2,1)S(1)}, u32[]{:S(2)}, u32[]{:S(2)}) collective-permute-start(bf16[784,768]{1,0:T(8,128)(2,1)S(1)} %add_convert_fusion.4), channel_id=1, source_target_pairs={{0,1},{1,2},{2,3},{3,0},{4,5},{5,6},{6,7},{7,4},{8,9},{9,10},{10,1... | collective-permute-start | bytes 3612680 | tf_op jit(solution)/shard_map/ppermute | solution.py:32
  327.6 55.5 %collective-permute-start.5 = (bf16[784,768]{1,0:T(8,128)(2,1)S(1)}, bf16[784,768]{1,0:T(8,128)(2,1)S(1)}, u32[]{:S(2)}, u32[]{:S(2)}) collective-permute-start(bf16[784,768]{1,0:T(8,128)(2,1)S(1)} %add_convert_fusion.4), channel_id=1, source_target_pairs={{1,0},{2,1},{3,2},{0,3},{5,4},{6,5},{7,6},{4,7},{9,8},{10,9},{11,1... | collective-permute-start | bytes 3612680 | tf_op jit(solution)/shard_map/ppermute | solution.py:35
  357.4 50.2 %collective-permute-start.4 = (bf16[784,768]{1,0:T(8,128)(2,1)S(1)}, bf16[784,768]{1,0:T(8,128)(2,1)S(1)}, u32[]{:S(2)}, u32[]{:S(2)}) collective-permute-start(bf16[784,768]{1,0:T(8,128)(2,1)S(1)} %collective-permute-done.3), channel_id=1, source_target_pairs={{0,1},{1,2},{2,3},{3,0},{4,5},{5,6},{6,7},{7,4},{8,9},{9,10},{10,1... | collective-permute-start | bytes 3612680 | tf_op jit(solution)/shard_map/ppermute | solution.py:32
  578.6 524.3 %reduce-scatter.13.cloned.1.call-start = ((), (), s32[]{:S(2)}) async-start(), calls=%async_computation.13 | async-start | bytes 12042240 | tf_op jit(solution)/shard_map/reduce_scatter | solution.py:135
  582.4 192.8 %collective-permute-start.9 = (bf16[784,768]{1,0:T(8,128)(2,1)S(1)}, bf16[784,768]{1,0:T(8,128)(2,1)}, u32[]{:S(2)}, u32[]{:S(2)}) collective-permute-start(bf16[784,768]{1,0:T(8,128)(2,1)S(1)} %reshape.457), channel_id=1, source_target_pairs={{0,1},{1,2},{2,3},{3,0},{4,5},{5,6},{6,7},{7,4},{8,9},{9,10},{10,1... | collective-permute-start | bytes 3612680 | tf_op jit(solution)/shard_map/ppermute | solution.py:32
  769.9 60.5 %copy-start.78 = (bf16[768]{0:T(1024)(128)(2,1)S(1)}, bf16[768]{0:T(1024)(128)(2,1)}, u32[]{:S(2)}) copy-start(bf16[768]{0:T(1024)(128)(2,1)} %param.36) | copy-start | bytes 4612
  771.4 31.5 %collective-permute-start.6 = (bf16[784,768]{1,0:T(8,128)(2,1)}, bf16[784,768]{1,0:T(8,128)(2,1)}, u32[]{:S(2)}, u32[]{:S(2)}) collective-permute-start(bf16[784,768]{1,0:T(8,128)(2,1)} %add_convert_fusion.3), channel_id=1, source_target_pairs={{0,1},{1,2},{2,3},{3,0},{4,5},{5,6},{6,7},{7,4},{8,9},{9,10},{10,1... | collective-permute-start | bytes 3612680 | tf_op jit(solution)/shard_map/ppermute | solution.py:32
  772.9 57.6 %collective-permute-start.11 = (bf16[784,768]{1,0:T(8,128)(2,1)S(1)}, bf16[784,768]{1,0:T(8,128)(2,1)}, u32[]{:S(2)}, u32[]{:S(2)}) collective-permute-start(bf16[784,768]{1,0:T(8,128)(2,1)S(1)} %reshape.457), channel_id=1, source_target_pairs={{1,0},{2,1},{3,2},{0,3},{5,4},{6,5},{7,6},{4,7},{9,8},{10,9},{11,1... | collective-permute-start | bytes 3612680 | tf_op jit(solution)/shard_map/ppermute | solution.py:35
  775.2 79.4 %collective-permute-start.10 = (bf16[784,768]{1,0:T(8,128)(2,1)}, bf16[784,768]{1,0:T(8,128)(2,1)}, u32[]{:S(2)}, u32[]{:S(2)}) collective-permute-start(bf16[784,768]{1,0:T(8,128)(2,1)} %collective-permute-done.9), channel_id=1, source_target_pairs={{0,1},{1,2},{2,3},{3,0},{4,5},{5,6},{6,7},{7,4},{8,9},{9,10},{10,1... | collective-permute-start | bytes 3612680 | tf_op jit(solution)/shard_map/ppermute | solution.py:32
  775.2 105.0 %collective-permute-start.8 = (bf16[784,768]{1,0:T(8,128)(2,1)}, bf16[784,768]{1,0:T(8,128)(2,1)}, u32[]{:S(2)}, u32[]{:S(2)}) collective-permute-start(bf16[784,768]{1,0:T(8,128)(2,1)} %add_convert_fusion.3), channel_id=1, source_target_pairs={{1,0},{2,1},{3,2},{0,3},{5,4},{6,5},{7,6},{4,7},{9,8},{10,9},{11,1... | collective-permute-start | bytes 3612680 | tf_op jit(solution)/shard_map/ppermute | solution.py:35
  802.9 101.9 %collective-permute-start.7 = (bf16[784,768]{1,0:T(8,128)(2,1)}, bf16[784,768]{1,0:T(8,128)(2,1)}, u32[]{:S(2)}, u32[]{:S(2)}) collective-permute-start(bf16[784,768]{1,0:T(8,128)(2,1)} %collective-permute-done.6), channel_id=1, source_target_pairs={{0,1},{1,2},{2,3},{3,0},{4,5},{5,6},{6,7},{7,4},{8,9},{9,10},{10,1... | collective-permute-start | bytes 3612680 | tf_op jit(solution)/shard_map/ppermute | solution.py:32
  909.9 13.7 slice-start.4
  939.9 330.6 %reduce-scatter.11.cloned.1.call-start = ((), (), s32[]{:S(2)}) async-start(), calls=%async_computation.12 | async-start | bytes 12042240 | tf_op jit(solution)/shard_map/reduce_scatter | solution.py:135
  1277.0 31.2 %collective-permute-start.12 = (bf16[784,768]{1,0:T(8,128)(2,1)S(1)}, bf16[784,768]{1,0:T(8,128)(2,1)S(1)}, u32[]{:S(2)}, u32[]{:S(2)}) collective-permute-start(bf16[784,768]{1,0:T(8,128)(2,1)S(1)} %get-tuple-element.150), channel_id=1, source_target_pairs={{0,1},{1,2},{2,3},{3,0},{4,5},{5,6},{6,7},{7,4},{8,9},{9,10},{10,1... | collective-permute-start | bytes 3612680 | tf_op jit(solution)/shard_map/ppermute | solution.py:32
  1278.5 55.4 %collective-permute-start.14 = (bf16[784,768]{1,0:T(8,128)(2,1)S(1)}, bf16[784,768]{1,0:T(8,128)(2,1)S(1)}, u32[]{:S(2)}, u32[]{:S(2)}) collective-permute-start(bf16[784,768]{1,0:T(8,128)(2,1)S(1)} %get-tuple-element.150), channel_id=1, source_target_pairs={{1,0},{2,1},{3,2},{0,3},{5,4},{6,5},{7,6},{4,7},{9,8},{10,9},{11,1... | collective-permute-start | bytes 3612680 | tf_op jit(solution)/shard_map/ppermute | solution.py:35
  1308.3 50.2 %collective-permute-start.13 = (bf16[784,768]{1,0:T(8,128)(2,1)S(1)}, bf16[784,768]{1,0:T(8,128)(2,1)S(1)}, u32[]{:S(2)}, u32[]{:S(2)}) collective-permute-start(bf16[784,768]{1,0:T(8,128)(2,1)S(1)} %collective-permute-done.12), channel_id=1, source_target_pairs={{0,1},{1,2},{2,3},{3,0},{4,5},{5,6},{6,7},{7,4},{8,9},{9,10},{10,1... | collective-permute-start | bytes 3612680 | tf_op jit(solution)/shard_map/ppermute | solution.py:32
  1382.6 25.7 %all-to-all-start.2 = ((bf16[2,1568,192]{2,0,1:T(2,128)(2,1)}), bf16[2,1568,192]{2,0,1:T(2,128)(2,1)}, u32[]{:S(2)}, u32[]{:S(2)}) async-start(bf16[2,1568,192]{2,0,1:T(2,128)(2,1)} %copy.184), calls=%async_computation.6 | async-start | bytes 3211264 | tf_op jit(solution)/shard_map/all_to_all | solution.py:146
  1386.9 300.2 %reduce-scatter.15.cloned.1.call-start = ((), (), s32[]{:S(2)}) async-start(), calls=%async_computation.14 | async-start | bytes 12042240 | tf_op jit(solution)/shard_map/reduce_scatter | solution.py:135
  1525.0 162.1 %copy-start.51 = (f32[784]{0:T(1024)S(1)}, f32[784]{0:T(1024)}, u32[]{:S(2)}) copy-start(f32[784]{0:T(1024)} %copy-done.50) | copy-start | bytes 9412
  1525.0 162.1 %copy-start.57 = (f32[784]{0:T(1024)S(1)}, f32[784]{0:T(1024)}, u32[]{:S(2)}) copy-start(f32[784]{0:T(1024)} %copy-done.56) | copy-start | bytes 9412
  1525.0 162.1 %copy-start.60 = (f32[768]{0:T(1024)S(1)}, f32[768]{0:T(1024)}, u32[]{:S(2)}) copy-start(f32[768]{0:T(1024)} %param.27) | copy-start | bytes 9220
  1525.0 165.5 %copy-start.64 = (f32[784]{0:T(1024)S(1)}, f32[784]{0:T(1024)}, u32[]{:S(2)}) copy-start(f32[784]{0:T(1024)} %copy-done.63) | copy-start | bytes 9412
  1525.0 495.3 %reduce-scatter.17.cloned.1.call-start = ((), (), s32[]{:S(2)}) async-start(), calls=%async_computation.15 | async-start | bytes 12042240 | tf_op jit(solution)/shard_map/reduce_scatter | solution.py:135
  1693.3 58.2 %copy-start.41 = (f32[16,3,196]{2,1,0:T(4,128)S(1)}, f32[16,3,196]{2,1,0:T(4,128)}, u32[]{:S(2)}) copy-start(f32[16,3,196]{2,1,0:T(4,128)} %copy-done.40) | copy-start | bytes 112900
  1693.4 58.2 %copy-start.49 = (f32[16,3,196]{2,1,0:T(4,128)S(1)}, f32[16,3,196]{2,1,0:T(4,128)}, u32[]{:S(2)}) copy-start(f32[16,3,196]{2,1,0:T(4,128)} %copy-done.48) | copy-start | bytes 112900
  1694.8 31.2 %collective-permute-start.15 = (bf16[784,768]{1,0:T(8,128)(2,1)S(1)}, bf16[784,768]{1,0:T(8,128)(2,1)S(1)}, u32[]{:S(2)}, u32[]{:S(2)}) collective-permute-start(bf16[784,768]{1,0:T(8,128)(2,1)S(1)} %get-tuple-element.152), channel_id=1, source_target_pairs={{0,1},{1,2},{2,3},{3,0},{4,5},{5,6},{6,7},{7,4},{8,9},{9,10},{10,1... | collective-permute-start | bytes 3612680 | tf_op jit(solution)/shard_map/ppermute | solution.py:32
  1696.3 55.4 %collective-permute-start.17 = (bf16[784,768]{1,0:T(8,128)(2,1)S(1)}, bf16[784,768]{1,0:T(8,128)(2,1)S(1)}, u32[]{:S(2)}, u32[]{:S(2)}) collective-permute-start(bf16[784,768]{1,0:T(8,128)(2,1)S(1)} %get-tuple-element.152), channel_id=1, source_target_pairs={{1,0},{2,1},{3,2},{0,3},{5,4},{6,5},{7,6},{4,7},{9,8},{10,9},{11,1... | collective-permute-start | bytes 3612680 | tf_op jit(solution)/shard_map/ppermute | solution.py:35
  1726.0 50.2 %collective-permute-start.16 = (bf16[784,768]{1,0:T(8,128)(2,1)S(1)}, bf16[784,768]{1,0:T(8,128)(2,1)S(1)}, u32[]{:S(2)}, u32[]{:S(2)}) collective-permute-start(bf16[784,768]{1,0:T(8,128)(2,1)S(1)} %collective-permute-done.15), channel_id=1, source_target_pairs={{0,1},{1,2},{2,3},{3,0},{4,5},{5,6},{6,7},{7,4},{8,9},{9,10},{10,1... | collective-permute-start | bytes 3612680 | tf_op jit(solution)/shard_map/ppermute | solution.py:32
  1856.4 309.9 %all-reduce.5.cloned.1.call-start = ((), (), s32[]{:S(2)}) async-start(), calls=%async_computation.16 | async-start | bytes 18874368 | tf_op jit(solution)/shard_map/psum | solution.py:337
  1856.5 19.2 slice-start.6
  1877.7 19.2 slice-start.2
  1884.4 12.6 slice-start.3
  1908.2 112.1 %copy-start.53 = (f32[784]{0:T(1024)S(1)}, f32[784]{0:T(1024)}, u32[]{:S(2)}) copy-start(f32[784]{0:T(1024)} %copy-done.52) | copy-start | bytes 9412
  1908.3 112.1 %copy-start.55 = (f32[784]{0:T(1024)S(1)}, f32[784]{0:T(1024)}, u32[]{:S(2)}) copy-start(f32[784]{0:T(1024)} %copy-done.54) | copy-start | bytes 9412
  1908.3 112.1 %copy-start.62 = (f32[768]{0:T(1024)S(1)}, f32[768]{0:T(1024)}, u32[]{:S(2)}) copy-start(f32[768]{0:T(1024)} %param.21) | copy-start | bytes 9220
  1925.3 98.5 %copy-start.66 = (f32[784]{0:T(1024)S(1)}, f32[784]{0:T(1024)}, u32[]{:S(2)}) copy-start(f32[784]{0:T(1024)} %copy-done.65) | copy-start | bytes 9412
  (71 other events, 275.2 us)
Sparse Core Ops, SparseCore 0:
  158.4 163.6 reduce-scatter.6
  578.7 187.6 reduce-scatter.8
  940.0 162.8 reduce-scatter.12
  1105.1 165.2 reduce-scatter.10
  1525.2 161.8 reduce-scatter.14
  1856.6 163.6 reduce-scatter.16
  2026.5 139.7 all-reduce.4
